TPU v7x, 256 devices: a whole 4x4x8 slice. The times are simulated.
256 devices in a mesh: row: 16 (over x, y), col: 16 (over z, core).
Axes of the slice: x: 4, y: 4, z: 8, core: 2. Of those that a mesh axis runs over, the one named last changes fastest.
Arguments:
- inputs: bfloat16 [2048, 16384], P('col', 'row'), may hold values from -6 to 6
- weight: bfloat16 [16384, 16384], P('row', 'col'), may hold values from -0.046875 to 0.046875
- cotangent: bfloat16 [2048, 16384], P('row', 'col'), may hold values from -0.75 to 0.75
- scale_in: float32 [8, 16384], P(None, 'row'), may hold values from -4 to 4
- scale_out: float32 [8, 16384], P(None, 'col'), may hold values from -4 to 4
- member: int32 [2048], replicated, may hold values from 0 to 7
Outputs:
- input_grad: bfloat16 [2048, 16384], P('col', 'row')
- weight_grad: float32 [16384, 16384], P('row', 'col')
- in_factor_grad: float32 [8, 16384], P(None, 'row')
- out_factor_grad: float32 [8, 16384], P(None, 'col')
All inputs are finite; a program needn't handle non-finite values.
Results may differ from a plain program's by a relative error of at most 0.0049.
Values may be sent and summed in bfloat16 or wider, within the bound.
No kernel may reach another device: no remote copies, remote signals or barrier semaphores. Data moves between devices by JAX's collectives and lax.ppermute only.
A program may use at most 128 MiB of HBM per device.

v0:
```python
import jax
import jax.numpy as jnp
from jax import lax
from jax.sharding import PartitionSpec as P

highest = lax.Precision.HIGHEST


def from_everyone(value, axis):
    copies = jnp.broadcast_to(value, (lax.axis_size(axis), *value.shape))
    return lax.all_to_all(copies, axis, split_axis=0, concat_axis=0, tiled=True)


def of_everyone(value, axis):
    return from_everyone(value, axis).sum(axis=0)


def gathered_total(value, axis):
    return lax.all_gather(value, axis).sum(0)


def member_sums(one_hot, values):
    return jnp.dot(one_hot.T, values, precision=highest)


def local(inputs, weight, cotangent, scale_in, scale_out, member):
    n_members = scale_in.shape[0]
    one_hot = (member[:, None] == jnp.arange(n_members, dtype=jnp.int32)[None, :]).astype(
        jnp.float32
    )
    full_inputs = lax.all_gather(inputs, "col", axis=0, tiled=True)
    full_cot = lax.all_gather(cotangent, "row", axis=0, tiled=True)
    r_rows = jnp.dot(one_hot, scale_in, precision=highest)
    s_rows = jnp.dot(one_hot, scale_out, precision=highest)
    scaled_in = (full_inputs * r_rows).astype(jnp.bfloat16)
    scaled_cot = (full_cot * s_rows).astype(jnp.bfloat16)
    batch = scaled_in.shape[0]
    pre_part = jnp.dot(scaled_in, weight, preferred_element_type=jnp.float32)
    out_term = member_sums(one_hot, full_cot.astype(jnp.float32) * pre_part)
    out_factor_grad = of_everyone(out_term, "row")
    col_share = batch // lax.axis_size("col")
    col_start = lax.axis_index("col") * col_share
    back_part = lax.dot_general(
        scaled_cot, weight, (((1,), (1,)), ((), ())), preferred_element_type=jnp.float32
    )
    in_term = member_sums(one_hot, full_inputs.astype(jnp.float32) * back_part)
    in_factor_grad = gathered_total(in_term, "col")
    back_block = lax.psum_scatter(back_part, "col", scatter_dimension=0, tiled=True)
    r_block = lax.dynamic_slice_in_dim(r_rows, col_start, col_share, 0)
    input_grad = (back_block * r_block).astype(jnp.bfloat16)
    weight_grad = lax.dot_general(
        scaled_in, scaled_cot, (((0,), (0,)), ((), ())), preferred_element_type=jnp.float32
    )
    return (input_grad, weight_grad, in_factor_grad, out_factor_grad)


def solution(mesh):
    placed = (
        P("col", "row"),
        P("row", "col"),
        P("row", "col"),
        P(None, "row"),
        P(None, "col"),
        P(),
    )
    return jax.shard_map(
        local,
        mesh=mesh,
        in_specs=placed,
        out_specs=(P("col", "row"), P("row", "col"), P(None, "row"), P(None, "col")),
        check_vma=False,
    )
```

profile of v0, /device:TPU:2, one launch (start us, length us, event | category | flops | bytes accessed | tf_op | source)
XLA Modules:
  0.0 195.8 jit_solution(3907940686163401925)
XLA Ops:
  7.2 0.0 copy-start
  7.2 0.0 all-gather.4.cloned.1.call-start
  7.2 0.7 all-gather.4.cloned.1.call-update
  7.9 0.0 all-gather.6.cloned.1.call-start
  8.0 0.7 all-gather.6.cloned.1.call-update
  8.7 0.0 reduce-scatter.2.cloned.1.call-start
  8.7 61.1 %all-gather.4.cloned.1.call-done = bf16[2048,1024]{1,0:T(8,128)(2,1)} async-done(((bf16[128,1024]{1,0:T(8,128)(2,1)}), bf16[2048,1024]{1,0:T(8,128)(2,1)}) %all-gather.4.cloned.1.call-update) | async-done | bytes 4194320 | tf_op jit(solution)/shard_map/all_gather | solution.py:32
  69.8 5.6 %fusion = bf16[2048,1024]{1,0:T(8,128)(2,1)S(1)} fusion(bf16[2048,1024]{1,0:T(8,128)(2,1)} %all-gather.4.cloned.1.call-done, f32[8,1024]{1,0:T(8,128)} %param.10, s32[2048]{0:T(1024)} %param.11), kind=kOutput, calls=%fused_computation.4 | convolution fusion | flops 207634432 | bytes 8429568 | tf_op jit(solution)/shard_map/dot_general | solution.py:34
  75.4 0.0 copy-start.2
  75.4 2.0 copy-done.2
  77.4 0.0 copy-done
  77.4 7.1 %fusion.13 = f32[2048,1024]{1,0:T(8,128)} fusion(bf16[2048,1024]{1,0:T(8,128)(2,1)S(1)} %fusion, bf16[1024,1024]{1,0:T(8,128)(2,1)S(1)} %copy-done), kind=kOutput, calls=%fused_computation.18 | convolution fusion | flops 4294967296 | bytes 14680064 | tf_op jit(solution)/shard_map/dot_general | solution.py:43
  84.4 0.0 copy-start.4
  84.4 0.0 copy-start.5
  84.4 0.0 reduce-scatter.2.cloned.1.call-update
  84.5 0.7 copy-done.4
  85.1 0.1 copy-done.5
  85.2 5.6 %fusion.4 = f32[2048,1024]{1,0:T(8,128)} fusion(f32[8,1024]{1,0:T(8,128)S(1)} %copy-done.5, s32[2048]{0:T(1024)S(1)} %copy-done.4), kind=kOutput, calls=%fused_computation.9 | convolution fusion | flops 201342976 | bytes 8429568 | tf_op jit(solution)/shard_map/dot_general | solution.py:33
  90.8 22.5 %all-gather.6.cloned.1.call-done = bf16[2048,1024]{1,0:T(8,128)(2,1)} async-done(((bf16[128,1024]{1,0:T(8,128)(2,1)}), bf16[2048,1024]{1,0:T(8,128)(2,1)}) %all-gather.6.cloned.1.call-update) | async-done | bytes 4194320 | tf_op jit(solution)/shard_map/all_gather | solution.py:31
  113.3 0.0 copy-start.1
  113.3 7.7 %fusion.9 = f32[2048,1024]{1,0:T(8,128)S(1)} fusion(bf16[1024,1024]{1,0:T(8,128)(2,1)S(1)} %copy-done, f32[2048,1024]{1,0:T(8,128)} %fusion.4, bf16[2048,1024]{1,0:T(8,128)(2,1)} %all-gather.6.cloned.1.call-done), kind=kOutput, calls=%fused_computation.16 | convolution fusion | flops 4301258752 | bytes 23068672 | tf_op jit(solution)/shard_map/dot_general | solution.py:38
  121.0 0.0 copy-done.1
  121.0 3.4 %fusion.1 = f32[8,1024]{1,0:T(8,128)S(1)} fusion(f32[2048,1024]{1,0:T(8,128)S(1)} %fusion.9, bf16[2048,1024]{1,0:T(8,128)(2,1)S(1)} %copy-done.1, s32[2048]{0:T(1024)S(1)} %copy-done.4), kind=kOutput, calls=%fused_computation.5 | convolution fusion | flops 205537280 | bytes 12623872 | tf_op jit(solution)/shard_map/dot_general | solution.py:23
  124.5 0.9 broadcast_in_dim.2
  125.3 7.3 %all-to-all-start = ((f32[16,8,1024]{2,1,0:T(8,128)}), f32[16,8,1024]{2,1,0:T(8,128)S(1)}, u32[]{:S(2)}, u32[]{:S(2)}) async-start(f32[16,8,1024]{2,1,0:T(8,128)} %broadcast_in_dim.2), calls=%async_computation.1 | async-start | bytes 1048576 | tf_op jit(solution)/shard_map/all_to_all | solution.py:11
  132.6 0.0 copy-start.3
  132.6 12.9 %fusion.11 = f32[1024,1024]{1,0:T(8,128)} fusion(bf16[2048,1024]{1,0:T(8,128)(2,1)} %copy-done.2, f32[2048,1024]{1,0:T(8,128)} %fusion.4, bf16[2048,1024]{1,0:T(8,128)(2,1)} %all-gather.6.cloned.1.call-done), kind=kOutput, calls=%fused_computation.17 | convolution fusion | flops 4301258752 | bytes 20971520 | tf_op jit(solution)/shard_map/dot_general | solution.py:51
  145.5 0.0 copy-done.3
  145.5 5.9 %fusion.3 = f32[8,1024]{1,0:T(8,128)S(1)} fusion(f32[2048,1024]{1,0:T(8,128)} %fusion.13, bf16[2048,1024]{1,0:T(8,128)(2,1)S(1)} %copy-done.3, s32[2048]{0:T(1024)S(1)} %copy-done.4), kind=kOutput, calls=%fused_computation.7 | convolution fusion | flops 205537280 | bytes 12623872 | tf_op jit(solution)/shard_map/dot_general | solution.py:23
  151.4 18.8 %all-gather = f32[128,1024]{1,0:T(8,128)S(1)} all-gather(f32[8,1024]{1,0:T(8,128)S(1)} %fusion.3), channel_id=2, replica_groups=mesh['row'=16,'col'=16] {'col'}, dimensions={0}, use_global_device_ids=true | all-gather | bytes 557056 | tf_op jit(solution)/shard_map/all_gather | solution.py:19
  170.2 0.6 bitcast_reduce_fusion
  170.9 0.0 all-to-all-done
  170.9 0.6 reduce_sum.19
  171.5 15.8 %reduce-scatter.2.cloned.1.call-done = f32[128,1024]{1,0:T(8,128)} async-done(((f32[2048,1024]{1,0:T(8,128)}), f32[128,1024]{1,0:T(8,128)}) %reduce-scatter.2.cloned.1.call-update) | async-done | bytes 524304 | tf_op jit(solution)/shard_map/reduce_scatter | solution.py:48
  187.4 2.0 %multiply_convert_fusion = bf16[128,1024]{1,0:T(8,128)(2,1)} fusion(f32[128,1024]{1,0:T(8,128)} %reduce-scatter.2.cloned.1.call-done, f32[2048,1024]{1,0:T(8,128)} %fusion.4, s32[]{:T(128)S(6)} %select_n.3), kind=kLoop, calls=%fused_computation.11 | loop fusion | flops 262144 | bytes 1310724 | tf_op jit(solution)/shard_map/convert_element_type | solution.py:50
Async XLA Ops:
  7.2 70.2 %copy-start = (bf16[1024,1024]{1,0:T(8,128)(2,1)S(1)}, bf16[1024,1024]{1,0:T(8,128)(2,1)}, u32[]{:S(2)}) copy-start(bf16[1024,1024]{1,0:T(8,128)(2,1)} %param.7) | copy-start | bytes 6291460
  7.2 62.6 %all-gather.4.cloned.1.call-start = ((), (), s32[]{:S(2)}) async-start(), calls=%async_computation.2 | async-start | bytes 4456448 | tf_op jit(solution)/shard_map/all_gather | solution.py:32
  7.9 105.4 %all-gather.6.cloned.1.call-start = ((), (), s32[]{:S(2)}) async-start(), calls=%async_computation.4 | async-start | bytes 4456448 | tf_op jit(solution)/shard_map/all_gather | solution.py:31
  8.7 178.7 %reduce-scatter.2.cloned.1.call-start = ((), (), s32[]{:S(2)}) async-start(), calls=%async_computation.3 | async-start | bytes 8912896 | tf_op jit(solution)/shard_map/reduce_scatter | solution.py:48
  75.4 2.0 %copy-start.2 = (bf16[2048,1024]{1,0:T(8,128)(2,1)}, bf16[2048,1024]{1,0:T(8,128)(2,1)S(1)}, u32[]{:S(2)}) copy-start(bf16[2048,1024]{1,0:T(8,128)(2,1)S(1)} %fusion) | copy-start | bytes 12582916
  84.4 0.7 copy-start.4
  84.4 0.8 copy-start.5
  113.3 7.7 %copy-start.1 = (bf16[2048,1024]{1,0:T(8,128)(2,1)S(1)}, bf16[2048,1024]{1,0:T(8,128)(2,1)}, u32[]{:S(2)}) copy-start(bf16[2048,1024]{1,0:T(8,128)(2,1)} %all-gather.4.cloned.1.call-done) | copy-start | bytes 12582916
  125.3 45.5 %all-to-all-start = ((f32[16,8,1024]{2,1,0:T(8,128)}), f32[16,8,1024]{2,1,0:T(8,128)S(1)}, u32[]{:S(2)}, u32[]{:S(2)}) async-start(f32[16,8,1024]{2,1,0:T(8,128)} %broadcast_in_dim.2), calls=%async_computation.1 | async-start | bytes 1048576 | tf_op jit(solution)/shard_map/all_to_all | solution.py:11
  132.6 12.9 %copy-start.3 = (bf16[2048,1024]{1,0:T(8,128)(2,1)S(1)}, bf16[2048,1024]{1,0:T(8,128)(2,1)}, u32[]{:S(2)}) copy-start(bf16[2048,1024]{1,0:T(8,128)(2,1)} %all-gather.6.cloned.1.call-done) | copy-start | bytes 12582916
Sparse Core Ops, SparseCore 0:
  10.4 59.3 all-gather.3
  71.7 41.6 all-gather.5
  115.9 71.4 reduce-scatter.1
where the time goes:
time: 196 us
  waiting for transfers between devices  101 us (52%)
  matrix products  48.2 us (25%)
  blocking collectives  18.8 us (10%)
  between operations  13.8 us (7%)
  starting transfers between devices  7.39 us (4%)
  local copies, waits for them, and re-layouts  3.59 us (2%)
  other arithmetic  3.25 us (2%)
    all_gather x1, waiting for transfers between devices, local(): full_cot = lax.all_gather(cotangent, 'row', axis=0, tiled=True)  61.1 us
    all_gather x1, waiting for transfers between devices, local(): full_inputs = lax.all_gather(inputs, 'col', axis=0, tiled=True)  22.5 us
    all_gather x1, blocking collectives, gathered_total(): return lax.all_gather(value, axis).sum(0)  18.8 us
    reduce_scatter x1, waiting for transfers between devices, local(): lax.psum_scatter(back_part, 'col', scatter_dimension=0, tiled=True)  15.8 us
    dot_general x1, matrix products, local(): lax.dot_general(scaled_in, scaled_cot, (((0,), (0,)), ((), ())), preferre...  12.9 us
    dot_general x2, matrix products, member_sums(): return jnp.dot(one_hot.T, values, precision=highest)  9.29 us
    dot_general x1, matrix products, local(): pre_part = jnp.dot(scaled_in, weight, preferred_element_type=jnp.float32)  7.7 us
    all_to_all x1, starting transfers between devices, from_everyone(): return lax.all_to_all(copies, axis, split_axis=0, concat_axis=0, tiled=True)  7.28 us
  transfers between devices with their start and end apart: 4, of which 3 were waited for; matrix products, arithmetic and copies ran while one was open for 26% of the time, Pallas kernels for 0%

commit v1 on v0

--- a/solution.py
+++ b/solution.py
@@ -29,7 +29,15 @@
         jnp.float32
     )
     full_inputs = lax.all_gather(inputs, "col", axis=0, tiled=True)
-    full_cot = lax.all_gather(cotangent, "row", axis=0, tiled=True)
+    full_cot = jnp.concatenate(
+        lax.all_to_all(
+            jnp.stack([cotangent for _ in range(lax.axis_size("row"))]),
+            axis_name="row",
+            split_axis=0,
+            concat_axis=0,
+        ),
+        axis=0,
+    )
     r_rows = jnp.dot(one_hot, scale_in, precision=highest)
     s_rows = jnp.dot(one_hot, scale_out, precision=highest)
     scaled_in = (full_inputs * r_rows).astype(jnp.bfloat16)

time: 196 us -> 164 us (0.84)
  waiting for transfers between devices: 101 us -> 7.34 us
  blocking collectives: 18.8 us -> 79.3 us
  local copies, waits for them, and re-layouts: 3.59 us -> 7.11 us
    all_gather x1 -> x0, waiting for transfers between devices: 61.1 us -> none  [local(): full_cot = lax.all_gather(cotangent, 'row', axis=0, tiled=True)]
    all_to_all x0 -> x1, blocking collectives: none -> 56.6 us  [local(): lax.all_to_all(jnp.stack([cotangent for _ in range(lax.axis_size('row'))]...]
    all_gather x1, waiting for transfers between devices: 22.5 us -> 0.01 us  [local(): full_inputs = lax.all_gather(inputs, 'col', axis=0, tiled=True)]
    reduce_scatter x1, waiting for transfers between devices: 15.8 us -> 6.64 us  [local(): lax.psum_scatter(back_part, 'col', scatter_dimension=0, tiled=True)]
    all_gather x1, blocking collectives: 18.8 us -> 22.6 us  [gathered_total(): return lax.all_gather(value, axis).sum(0)]
    unnamed x12 -> x16, local copies, waits for them, and re-layouts: 2.71 us -> 4.75 us
  transfers between devices with their start and end apart: 4 -> 3, of which waited for: 3 -> 1; matrix products, arithmetic and copies ran while one was open for 26% -> 31% of each run, Pallas kernels for 0% -> 0%
where the time goes in v1:
time: 164 us
  blocking collectives  79.3 us (48%)
  matrix products  46.8 us (29%)
  between operations  14.1 us (9%)
  waiting for transfers between devices  7.34 us (4%)
  local copies, waits for them, and re-layouts  7.11 us (4%)
  starting transfers between devices  5.95 us (4%)
  other arithmetic  3.25 us (2%)
    all_to_all x1, blocking collectives, local(): lax.all_to_all(jnp.stack([cotangent for _ in range(lax.axis_size('row'))]...  56.6 us
    all_gather x1, blocking collectives, gathered_total(): return lax.all_gather(value, axis).sum(0)  22.6 us
    dot_general x1, matrix products, local(): lax.dot_general(scaled_in, scaled_cot, (((0,), (0,)), ((), ())), preferre...  13 us
    dot_general x2, matrix products, member_sums(): return jnp.dot(one_hot.T, values, precision=highest)  9.24 us
    dot_general x1, matrix products, local(): pre_part = jnp.dot(scaled_in, weight, preferred_element_type=jnp.float32)  7.7 us
    dot_general x1, matrix products, local(): lax.dot_general(scaled_cot, weight, (((1,), (1,)), ((), ())), preferred_e...  7.13 us
    reduce_scatter x1, waiting for transfers between devices, local(): lax.psum_scatter(back_part, 'col', scatter_dimension=0, tiled=True)  6.64 us
    all_to_all x1, starting transfers between devices, from_everyone(): return lax.all_to_all(copies, axis, split_axis=0, concat_axis=0, tiled=True)  5.87 us
  transfers between devices with their start and end apart: 3, of which 1 were waited for; matrix products, arithmetic and copies ran while one was open for 31% of the time, Pallas kernels for 0%

profile of v1, /device:TPU:2, one launch (start us, length us, event | category | flops | bytes accessed | tf_op | source)
XLA Modules:
  0.0 163.8 jit_solution(17665908159831454993)
XLA Ops:
  7.2 0.0 copy-start
  7.2 0.0 all-gather.3.cloned.1.call-start
  7.2 0.7 all-gather.3.cloned.1.call-update
  7.9 0.0 reduce-scatter.2.cloned.1.call-start
  8.0 1.5 stack.2
  9.4 0.0 copy-start.5
  9.5 0.0 copy-start.6
  9.5 56.6 %all_to_all.10 = bf16[16,128,1024]{2,1,0:T(8,128)(2,1)S(1)} all-to-all(bf16[16,128,1024]{2,1,0:T(8,128)(2,1)S(1)} %stack.2), channel_id=1, replica_groups=mesh['row'=16,'col'=16] {'row'}, dimensions={0} | all-to-all | bytes 8388608 | tf_op jit(solution)/shard_map/all_to_all | solution.py:33
  66.1 0.0 copy-start.1
  66.1 2.0 %copy-done.1 = bf16[16,128,1024]{2,1,0:T(8,128)(2,1)} copy-done((bf16[16,128,1024]{2,1,0:T(8,128)(2,1)}, bf16[16,128,1024]{2,1,0:T(8,128)(2,1)S(1)}, u32[]{:S(2)}) %copy-start.1) | copy-done | bytes 4194328
  68.1 0.0 copy-done.5
  68.1 0.0 copy-done.6
  68.1 4.0 %fusion.2 = bf16[2048,1024]{1,0:T(8,128)(2,1)S(1)} fusion(bf16[2048,1024]{1,0:T(8,128)(2,1)S(1)} %bitcast.10, f32[8,1024]{1,0:T(8,128)S(1)} %copy-done.6, s32[2048]{0:T(1024)S(1)} %copy-done.5), kind=kOutput, calls=%fused_computation.6 | convolution fusion | flops 207634432 | bytes 8429568 | tf_op jit(solution)/shard_map/dot_general | solution.py:42
  72.2 0.0 copy-start.3
  72.2 2.0 %copy-done.3 = bf16[2048,1024]{1,0:T(8,128)(2,1)} copy-done((bf16[2048,1024]{1,0:T(8,128)(2,1)}, bf16[2048,1024]{1,0:T(8,128)(2,1)S(1)}, u32[]{:S(2)}) %copy-start.3) | copy-done | bytes 4194328
  74.1 0.0 copy-done
  74.2 7.1 %fusion.13 = f32[2048,1024]{1,0:T(8,128)} fusion(bf16[2048,1024]{1,0:T(8,128)(2,1)S(1)} %fusion.2, bf16[1024,1024]{1,0:T(8,128)(2,1)S(1)} %copy-done), kind=kOutput, calls=%fused_computation.18 | convolution fusion | flops 4294967296 | bytes 14680064 | tf_op jit(solution)/shard_map/dot_general | solution.py:51
  81.3 0.0 copy-start.7
  81.3 0.0 reduce-scatter.2.cloned.1.call-update
  81.3 0.7 copy-done.7
  82.0 5.6 %fusion.4 = f32[2048,1024]{1,0:T(8,128)} fusion(f32[8,1024]{1,0:T(8,128)S(1)} %copy-done.7, s32[2048]{0:T(1024)S(1)} %copy-done.5), kind=kOutput, calls=%fused_computation.9 | convolution fusion | flops 201342976 | bytes 8429568 | tf_op jit(solution)/shard_map/dot_general | solution.py:41
  87.7 0.0 all-gather.3.cloned.1.call-done
  87.7 0.0 copy-start.2
  87.7 7.7 %fusion.9 = f32[2048,1024]{1,0:T(8,128)S(1)} fusion(bf16[1024,1024]{1,0:T(8,128)(2,1)S(1)} %copy-done, f32[2048,1024]{1,0:T(8,128)} %fusion.4, bf16[2048,1024]{1,0:T(8,128)(2,1)} %all-gather.3.cloned.1.call-done), kind=kOutput, calls=%fused_computation.16 | convolution fusion | flops 4301258752 | bytes 23068672 | tf_op jit(solution)/shard_map/dot_general | solution.py:46
  95.4 0.0 copy-done.2
  95.4 3.4 %fusion.3 = f32[8,1024]{1,0:T(8,128)S(1)} fusion(f32[2048,1024]{1,0:T(8,128)S(1)} %fusion.9, bf16[2048,1024]{1,0:T(8,128)(2,1)S(1)} %bitcast.11, s32[2048]{0:T(1024)S(1)} %copy-done.5), kind=kOutput, calls=%fused_computation.7 | convolution fusion | flops 205537280 | bytes 12623872 | tf_op jit(solution)/shard_map/dot_general | solution.py:23
  98.8 0.9 broadcast_in_dim.2
  99.7 5.9 %all-to-all-start.1 = ((f32[16,8,1024]{2,1,0:T(8,128)}), f32[16,8,1024]{2,1,0:T(8,128)S(1)}, u32[]{:S(2)}, u32[]{:S(2)}) async-start(f32[16,8,1024]{2,1,0:T(8,128)} %broadcast_in_dim.2), calls=%async_computation.2 | async-start | bytes 1048576 | tf_op jit(solution)/shard_map/all_to_all | solution.py:11
  105.6 0.0 copy-start.4
  105.6 13.0 %fusion.11 = f32[1024,1024]{1,0:T(8,128)} fusion(bf16[2048,1024]{1,0:T(8,128)(2,1)} %copy-done.3, f32[2048,1024]{1,0:T(8,128)} %fusion.4, bf16[2048,1024]{1,0:T(8,128)(2,1)} %all-gather.3.cloned.1.call-done), kind=kOutput, calls=%fused_computation.17 | convolution fusion | flops 4301258752 | bytes 20971520 | tf_op jit(solution)/shard_map/dot_general | solution.py:59
  118.6 0.0 copy-done.4
  118.6 5.8 %fusion.1 = f32[8,1024]{1,0:T(8,128)S(1)} fusion(f32[2048,1024]{1,0:T(8,128)} %fusion.13, bf16[2048,1024]{1,0:T(8,128)(2,1)S(1)} %copy-done.4, s32[2048]{0:T(1024)S(1)} %copy-done.5), kind=kOutput, calls=%fused_computation.5 | convolution fusion | flops 205537280 | bytes 12623872 | tf_op jit(solution)/shard_map/dot_general | solution.py:23
  124.4 22.6 %all-gather = f32[128,1024]{1,0:T(8,128)S(1)} all-gather(f32[8,1024]{1,0:T(8,128)S(1)} %fusion.1), channel_id=2, replica_groups=mesh['row'=16,'col'=16] {'col'}, dimensions={0}, use_global_device_ids=true | all-gather | bytes 557056 | tf_op jit(solution)/shard_map/all_gather | solution.py:19
  147.1 0.6 bitcast_reduce_fusion
  147.7 0.0 all-to-all-done.1
  147.7 0.6 reduce_sum.19
  148.4 6.6 %reduce-scatter.2.cloned.1.call-done = f32[128,1024]{1,0:T(8,128)} async-done(((f32[2048,1024]{1,0:T(8,128)}), f32[128,1024]{1,0:T(8,128)}) %reduce-scatter.2.cloned.1.call-update) | async-done | bytes 524304 | tf_op jit(solution)/shard_map/reduce_scatter | solution.py:56
  155.0 2.0 %multiply_convert_fusion = bf16[128,1024]{1,0:T(8,128)(2,1)} fusion(f32[128,1024]{1,0:T(8,128)} %reduce-scatter.2.cloned.1.call-done, f32[2048,1024]{1,0:T(8,128)} %fusion.4, s32[]{:T(128)S(6)} %select_n.3), kind=kLoop, calls=%fused_computation.11 | loop fusion | flops 262144 | bytes 1310724 | tf_op jit(solution)/shard_map/convert_element_type | solution.py:58
Async XLA Ops:
  7.2 67.0 %copy-start = (bf16[1024,1024]{1,0:T(8,128)(2,1)S(1)}, bf16[1024,1024]{1,0:T(8,128)(2,1)}, u32[]{:S(2)}) copy-start(bf16[1024,1024]{1,0:T(8,128)(2,1)} %param.7) | copy-start | bytes 6291460
  7.2 80.5 %all-gather.3.cloned.1.call-start = ((), (), s32[]{:S(2)}) async-start(), calls=%async_computation.4 | async-start | bytes 4456448 | tf_op jit(solution)/shard_map/all_gather | solution.py:31
  7.9 147.1 %reduce-scatter.2.cloned.1.call-start = ((), (), s32[]{:S(2)}) async-start(), calls=%async_computation.3 | async-start | bytes 8912896 | tf_op jit(solution)/shard_map/reduce_scatter | solution.py:56
  9.4 58.7 %copy-start.5 = (s32[2048]{0:T(1024)S(1)}, s32[2048]{0:T(1024)}, u32[]{:S(2)}) copy-start(s32[2048]{0:T(1024)} %param.11) | copy-start | bytes 24580
  9.5 58.7 %copy-start.6 = (f32[8,1024]{1,0:T(8,128)S(1)}, f32[8,1024]{1,0:T(8,128)}, u32[]{:S(2)}) copy-start(f32[8,1024]{1,0:T(8,128)} %param.10) | copy-start | bytes 98308
  66.1 2.0 %copy-start.1 = (bf16[16,128,1024]{2,1,0:T(8,128)(2,1)}, bf16[16,128,1024]{2,1,0:T(8,128)(2,1)S(1)}, u32[]{:S(2)}) copy-start(bf16[16,128,1024]{2,1,0:T(8,128)(2,1)S(1)} %all_to_all.10) | copy-start | bytes 12582916
  72.2 2.0 %copy-start.3 = (bf16[2048,1024]{1,0:T(8,128)(2,1)}, bf16[2048,1024]{1,0:T(8,128)(2,1)S(1)}, u32[]{:S(2)}) copy-start(bf16[2048,1024]{1,0:T(8,128)(2,1)S(1)} %fusion.2) | copy-start | bytes 12582916
  81.3 0.8 copy-start.7
  87.7 7.7 %copy-start.2 = (bf16[16,128,1024]{2,1,0:T(8,128)(2,1)S(1)}, bf16[16,128,1024]{2,1,0:T(8,128)(2,1)}, u32[]{:S(2)}) copy-start(bf16[16,128,1024]{2,1,0:T(8,128)(2,1)} %copy-done.1) | copy-start | bytes 12582916
  99.7 48.0 %all-to-all-start.1 = ((f32[16,8,1024]{2,1,0:T(8,128)}), f32[16,8,1024]{2,1,0:T(8,128)S(1)}, u32[]{:S(2)}, u32[]{:S(2)}) async-start(f32[16,8,1024]{2,1,0:T(8,128)} %broadcast_in_dim.2), calls=%async_computation.2 | async-start | bytes 1048576 | tf_op jit(solution)/shard_map/all_to_all | solution.py:11
  105.6 13.1 %copy-start.4 = (bf16[2048,1024]{1,0:T(8,128)(2,1)S(1)}, bf16[2048,1024]{1,0:T(8,128)(2,1)}, u32[]{:S(2)}) copy-start(bf16[2048,1024]{1,0:T(8,128)(2,1)} %all-gather.3.cloned.1.call-done) | copy-start | bytes 12582916
Sparse Core Ops, SparseCore 0:
  9.8 44.9 all-gather.2
  81.4 73.5 reduce-scatter.1
